TPU v7x, 32 devices: a whole 2x2x4 slice. The times are simulated.
32 devices in a mesh: leaf: 2 (over core), row: 4 (over y, x), col: 4 (over z).
Axes of the slice: x: 2, y: 2, z: 4, core: 2. Of those that a mesh axis runs over, the one named last changes fastest.
Arguments:
- rhs_leaf: bfloat16 [2, 8, 64, 2048], P('leaf', None, None, 'col'), may hold values from -6 to 6
- dinv_leaf: bfloat16 [2, 8, 2048, 2048], P('leaf', None, 'row', 'col'), as said below
- panel_leaf: bfloat16 [2, 8, 1024, 2048], P('leaf', None, 'col', 'row'), may hold values from -0.0625 to 0.0625
- counts: int32 [2, 8], P('leaf'), may hold values from 256 to 2048, as said below
- row_index: int32 [2, 8, 1024], P('leaf'), may hold values from 0 to 4095, as said below
- rhs_root: bfloat16 [64, 4096], P(None, 'col'), may hold values from -6 to 6
- dinv_root: bfloat16 [4096, 4096], P(('leaf', 'row')), as said below
Outputs:
- y_leaf: bfloat16 [2, 8, 64, 2048], P('leaf', None, None, 'row')
- y_root: bfloat16 [64, 4096], P(None, ('leaf', 'row'))
Inputs may be any that keep to these rules, and one draw needn't show every extreme that they name: `counts`: each subtree supernode has at least 256 columns; at least one supernode of every draw has all 2048. `row_index`: within one supernode the 1024 entries are distinct and increasing. `dinv_leaf`: each [2048, 2048] block is lower triangular with a nonzero diagonal. `dinv_root`: lower triangular with a nonzero diagonal.
All inputs are finite; a program needn't handle non-finite values.
Results may differ from a plain program's by a relative error of at most 0.0053.
Values may be sent and summed in bfloat16 or wider, within the bound.
No kernel may reach another device: no remote copies, remote signals or barrier semaphores. Data moves between devices by JAX's collectives and lax.ppermute only.
A program may use at most 64 MiB of HBM per device.

v0:
```python
import jax
import jax.numpy as jnp
from jax import lax
from jax.sharding import PartitionSpec as P


def local(rhs_leaf, dinv_leaf, panel_leaf, counts, row_index, rhs_root, dinv_root):
    width_col = rhs_leaf.shape[3]
    width_row = dinv_leaf.shape[2]
    panel_rows = panel_leaf.shape[2]
    columns = rhs_root.shape[0]
    sep_width = rhs_root.shape[1] * lax.axis_size("col")
    limit = counts[0][:, None, None]
    col_slots = lax.axis_index("col") * width_col + lax.iota(jnp.int32, width_col)
    masked = jnp.where(col_slots[None, None, :] < limit, rhs_leaf[0], jnp.zeros((), jnp.bfloat16))
    partial_value = jnp.einsum(
        "kbj,kij->kbi", masked, dinv_leaf[0], preferred_element_type=jnp.float32
    )
    summed = lax.psum(partial_value, "col")
    row_slots = lax.axis_index("row") * width_row + lax.iota(jnp.int32, width_row)
    live_rows = (row_slots[None, None, :] < limit).astype(jnp.float32)
    solved = (summed * live_rows).astype(jnp.bfloat16)
    update = jnp.einsum("kbi,kri->kbr", solved, panel_leaf[0], preferred_element_type=jnp.float32)
    offset = lax.axis_index("col") * panel_rows
    targets = lax.dynamic_slice_in_dim(row_index[0], offset, panel_rows, 1)
    flat_update = jnp.transpose(update, (1, 0, 2)).reshape(columns, -1)
    accum = jnp.zeros((columns, sep_width), jnp.float32).at[:, targets.reshape(-1)].add(flat_update)
    piece = lax.psum_scatter(accum, "col", scatter_dimension=1, tiled=True)
    share = lax.psum(piece, ("leaf", "row"))
    reduced = (rhs_root.astype(jnp.float32) - share).astype(jnp.bfloat16)
    whole_reduced = lax.all_gather(reduced, "col", axis=1, tiled=True)
    y_root = jnp.dot(whole_reduced, dinv_root.T, preferred_element_type=jnp.float32).astype(
        jnp.bfloat16
    )
    return (solved[None], y_root)


def solution(mesh):
    in_specs = (
        P("leaf", None, None, "col"),
        P("leaf", None, "row", "col"),
        P("leaf", None, "col", "row"),
        P("leaf", None),
        P("leaf", None, None),
        P(None, "col"),
        P(("leaf", "row"), None),
    )
    out_specs = (P("leaf", None, None, "row"), P(None, ("leaf", "row")))
    return jax.shard_map(local, mesh=mesh, in_specs=in_specs, out_specs=out_specs, check_vma=False)
```

profile of v0, /device:TPU:0, one launch (start us, length us, event | category | flops | bytes accessed | tf_op | source)
XLA Modules:
  0.0 218.8 jit_solution(5079778243573968000)
XLA Ops:
  7.2 0.0 copy-start
  7.2 0.0 all-reduce.3.cloned.1.call-start
  7.2 0.9 compare_convert_fusion
  8.1 4.7 %fusion = f32[8,64,512]{2,1,0:T(8,128)} fusion(bf16[1,8,512,512]{3,2,1,0:T(8,128)(2,1)} %param.8, bf16[1,8,64,512]{3,2,1,0:T(8,128)(2,1)} %param.7, pred[8,512]{1,0:T(8,128)(4,1)S(1)} %get-tuple-element.3), kind=kOutput, calls=%fused_computation.1 | convolution fusion | flops 268697600 | bytes 5771264 | tf_op jit(solution)/shard_map/kbj,kij->kbi/dot_general | solution.py:16
  12.8 0.0 all-reduce.3.cloned.1.call-update
  12.8 0.0 reduce-scatter.2.cloned.1.call-start
  12.9 0.7 dynamic-slice_bitcast_fusion
  13.6 54.0 %all-reduce.3.cloned.1.call-done = f32[8,64,512]{2,1,0:T(8,128)} async-done(((f32[8,64,512]{2,1,0:T(8,128)}), f32[8,64,512]{2,1,0:T(8,128)}) %all-reduce.3.cloned.1.call-update) | async-done | bytes 1048592 | tf_op jit(solution)/shard_map/psum | solution.py:19
  67.6 0.0 copy-done
  67.6 2.0 fusion.4
  69.6 0.1 copy.13
  69.7 1.3 copy.12
  71.0 13.3 %scatter_custom_fusion = f32[64,4096]{0,1:T(8,128)} fusion(s32[2048]{0:T(1024)S(1)} %bitcast.29, f32[2048,64]{1,0:T(8,128)} %copy.12, f32[]{:T(128)} %constant.7.clone.1), kind=kCustom, calls=%fused_computation.7 | custom fusion | flops 131072 | bytes 1049088 | tf_op jit(solution)/shard_map/scatter-add | solution.py:27
  84.3 0.0 reduce-scatter.2.cloned.1.call-update
  84.3 0.0 all-reduce.5.cloned.1.call-start
  84.4 0.0 copy-done.2
  84.4 0.2 copy.10
  84.6 42.8 %reduce-scatter.2.cloned.1.call-done = f32[64,1024]{0,1:T(8,128)} async-done(((f32[64,4096]{0,1:T(8,128)}), f32[64,1024]{0,1:T(8,128)}) %reduce-scatter.2.cloned.1.call-update) | async-done | bytes 262160 | tf_op jit(solution)/shard_map/reduce_scatter | solution.py:28
  127.4 0.0 all-reduce.5.cloned.1.call-update
  127.4 0.9 fusion.11
  128.4 56.2 %all-reduce.5.cloned.1.call-done = f32[64,1024]{0,1:T(8,128)} async-done(((f32[64,1024]{0,1:T(8,128)}), f32[64,1024]{0,1:T(8,128)}) %all-reduce.5.cloned.1.call-update) | async-done | bytes 262160 | tf_op jit(solution)/shard_map/psum | solution.py:29
  184.5 1.1 subtract_convert_fusion
  185.6 22.4 %all_gather.3 = bf16[64,4096]{0,1:T(8,128)(2,1)S(1)} all-gather(bf16[64,1024]{0,1:T(8,128)(2,1)S(1)} %subtract_convert_fusion), channel_id=1, replica_groups=mesh['leaf'=2,'row'=4,'col'=4] {'col'}, dimensions={1}, use_global_device_ids=true | all-gather | bytes 655360 | tf_op jit(solution)/shard_map/all_gather | solution.py:31
  208.0 4.2 %convolution_convert_fusion = bf16[64,512]{1,0:T(8,128)(2,1)} fusion(bf16[64,4096]{0,1:T(8,128)(2,1)S(1)} %all_gather.3, bf16[512,4096]{1,0:T(8,128)(2,1)} %param.13), kind=kOutput, calls=%fused_computation.6 | convolution fusion | flops 268468224 | bytes 4784128 | tf_op jit(solution)/shard_map/dot_general | solution.py:32
  (6 shorter events, 0.0 us)
Async XLA Ops:
  7.2 60.5 %copy-start = (bf16[1,8,256,512]{3,2,1,0:T(8,128)(2,1)S(1)}, bf16[1,8,256,512]{3,2,1,0:T(8,128)(2,1)}, u32[]{:S(2)}) copy-start(bf16[1,8,256,512]{3,2,1,0:T(8,128)(2,1)} %param.9) | copy-start | bytes 6291460
  7.2 60.4 %all-reduce.3.cloned.1.call-start = ((), (), s32[]{:S(2)}) async-start(), calls=%async_computation.1 | async-start | bytes 2097152 | tf_op jit(solution)/shard_map/psum | solution.py:19
  12.8 114.6 %reduce-scatter.2.cloned.1.call-start = ((), (), s32[]{:S(2)}) async-start(), calls=%async_computation.2 | async-start | bytes 2621440 | tf_op jit(solution)/shard_map/reduce_scatter | solution.py:28
  71.0 13.4 %copy-start.2 = (bf16[64,1024]{1,0:T(8,128)(2,1)S(1)}, bf16[64,1024]{1,0:T(8,128)(2,1)}, u32[]{:S(2)}) copy-start(bf16[64,1024]{1,0:T(8,128)(2,1)} %param.12) | copy-start | bytes 393220
  71.0 56.5 %copy-start.1 = (f32[8,64,512]{2,1,0:T(8,128)S(1)}, f32[8,64,512]{2,1,0:T(8,128)}, u32[]{:S(2)}) copy-start(f32[8,64,512]{2,1,0:T(8,128)} %all-reduce.3.cloned.1.call-done) | copy-start | bytes 3145732
  84.3 100.2 %all-reduce.5.cloned.1.call-start = ((), (), s32[]{:S(2)}) async-start(), calls=%async_computation.3 | async-start | bytes 1048576 | tf_op jit(solution)/shard_map/psum | solution.py:29
Sparse Core Ops, SparseCore 0:
  13.0 54.6 all-reduce.2
  84.5 42.8 reduce-scatter.1
  130.5 53.9 all-reduce.4
where the time goes:
time: 219 us
  waiting for transfers between devices  153 us (70%)
  blocking collectives  22.4 us (10%)
  other arithmetic  16.2 us (7%)
  between operations  13.8 us (6%)
  matrix products  10.9 us (5%)
  local copies, waits for them, and re-layouts  2.27 us (1%)
    psum x1, waiting for transfers between devices, local(): share = lax.psum(piece, ('leaf', 'row'))  56.2 us
    psum x1, waiting for transfers between devices, local(): summed = lax.psum(partial_value, 'col')  54 us
    reduce_scatter x1, waiting for transfers between devices, local(): piece = lax.psum_scatter(accum, 'col', scatter_dimension=1, tiled=True)  42.8 us
    all_gather x1, blocking collectives, local(): whole_reduced = lax.all_gather(reduced, 'col', axis=1, tiled=True)  22.4 us
    scatter-add x1, other arithmetic, local(): jnp.zeros((columns, sep_width), jnp.float32).at[:, targets.reshape(-1)]  13.3 us
    dot_general x1, matrix products, local(): jnp.einsum('kbj,kij->kbi', masked, dinv_leaf[0], preferred_element_type=j...  4.71 us
  transfers between devices with their start and end apart: 3, of which 3 were waited for; matrix products, arithmetic and copies ran while one was open for 1% of the time, Pallas kernels for 0%

commit v1 on v0

v1 whole, which is shorter than its diff:
```python
import functools

import jax
import jax.numpy as jnp
from jax import lax
from jax.experimental import pallas as pl
from jax.experimental.pallas import tpu as pltpu
from jax.sharding import PartitionSpec as P

LANES = 128
VMEM = pltpu.VMEM
SMEM = pltpu.SMEM
NT = (((1,), (1,)), ((), ()))


def shift(value, axis, step):
    size = lax.axis_size(axis)
    pairs = [(i, (i + step) % size) for i in range(size)]
    return lax.ppermute(value, axis, pairs)


def leaf_kernel(cols, counts_ref, x_ref, d_ref, *out_refs):
    node = pl.program_id(0)
    col = lax.axis_index("col")
    share = x_ref.shape[1] // cols
    width = x_ref.shape[2]
    limit = counts_ref[0, node] - col * width
    rows = []
    for step in range(cols):
        start = pl.multiple_of(lax.rem(col + step, cols) * share, share)
        rows.append(x_ref[0, pl.ds(start, share), :])
    x = jnp.concatenate(rows, axis=0)
    slots = lax.broadcasted_iota(jnp.int32, x.shape, 1)
    x = jnp.where(slots < limit, x, jnp.zeros_like(x))
    product = lax.dot_general(x, d_ref[0], NT, preferred_element_type=jnp.float32)
    for step, ref in enumerate(out_refs):
        ref[0] = product[step * share:(step + 1) * share].astype(ref.dtype)


def leaf_partials(cols, counts, rhs, dinv):
    nodes, columns, width = rhs.shape
    height = dinv.shape[1]
    share = columns // cols
    out = [jax.ShapeDtypeStruct((nodes, share, height), jnp.bfloat16 if step else jnp.float32)
           for step in range(cols)]
    return pl.pallas_call(
        functools.partial(leaf_kernel, cols),
        grid=(nodes,),
        in_specs=[
            pl.BlockSpec(memory_space=SMEM),
            pl.BlockSpec((1, columns, width), lambda i: (i, 0, 0)),
            pl.BlockSpec((1, height, width), lambda i: (i, 0, 0)),
        ],
        out_specs=[pl.BlockSpec((1, share, height), lambda i: (i, 0, 0)) for _ in out],
        out_shape=out,
        name="leaf_partials",
        cost_estimate=pl.CostEstimate(
            flops=2 * nodes * columns * width * height,
            bytes_accessed=2 * dinv.size, transcendentals=0),
    )(counts, rhs, dinv)


def solve_kernel(counts_ref, own_ref, *refs):
    *got_refs, out_ref = refs
    nodes, share, height = own_ref.shape
    base = lax.axis_index("row") * height
    for node in range(nodes):
        total = own_ref[node]
        for ref in got_refs:
            total = total + ref[node].astype(jnp.float32)
        slots = lax.broadcasted_iota(jnp.int32, total.shape, 1) + base
        total = jnp.where(slots < counts_ref[0, node], total, jnp.zeros_like(total))
        out_ref[node] = total.astype(out_ref.dtype)


def whole_vmem(count):
    return [pl.BlockSpec(memory_space=VMEM) for _ in range(count)]


def solve_rows(counts, own, got):
    return pl.pallas_call(
        solve_kernel,
        in_specs=[pl.BlockSpec(memory_space=SMEM)] + whole_vmem(1 + len(got)),
        out_specs=pl.BlockSpec(memory_space=VMEM),
        out_shape=jax.ShapeDtypeStruct(own.shape, jnp.bfloat16),
        name="solve_rows",
    )(counts, own, *got)


def join_kernel(direction, *refs):
    *in_refs, out_ref = refs
    cols = len(in_refs)
    share = in_refs[0].shape[-2]
    col = lax.axis_index("col")
    for step, ref in enumerate(in_refs):
        start = pl.multiple_of(lax.rem(col + cols - step, cols) * share, share)
        if len(ref.shape) == 3:
            out_ref[:, pl.ds(start, share), :] = ref[...]
        else:
            out_ref[pl.ds(start, share), :] = ref[...]


def join_columns(pieces):
    shape = list(pieces[0].shape)
    shape[-2] *= len(pieces)
    return pl.pallas_call(
        functools.partial(join_kernel, 0),
        in_specs=whole_vmem(len(pieces)),
        out_specs=pl.BlockSpec(memory_space=VMEM),
        out_shape=jax.ShapeDtypeStruct(tuple(shape), pieces[0].dtype),
        name="join_columns",
    )(*pieces)


def gather_kernel(cols, leaves, starts_ref, code_ref, *refs):
    value_refs, out_refs, table_ref = refs[:cols], refs[cols:-1], refs[-1]
    nodes, share, panel = value_refs[0].shape
    tiles = code_ref.shape[0]
    part = tiles // leaves
    col = lax.axis_index("col")
    leaf = lax.axis_index("leaf") if leaves > 1 else 0
    for step, ref in enumerate(value_refs):
        start = pl.multiple_of(lax.rem(col + step, cols) * panel, panel)
        table_ref[:, :, pl.ds(start, panel)] = ref[...].astype(jnp.float32)
    lane = lax.broadcasted_iota(jnp.int32, (share, LANES), 1)
    for step, out_ref in enumerate(out_refs):
        block = lax.rem(leaf + step, leaves)

        @pl.loop(0, part)
        def _(index):
            tile = block * part + index
            total = jnp.zeros((share, LANES), jnp.float32)
            codes = code_ref[tile]
            for node in range(nodes):
                first = starts_ref[node, tile]
                base = pl.multiple_of((first // LANES) * LANES, LANES)
                low = table_ref[node, :, pl.ds(base, LANES)]
                high = table_ref[node, :, pl.ds(base + LANES, LANES)]
                window = jnp.where(lane >= lax.rem(first, LANES), low, high)
                code = jnp.broadcast_to(codes[node:node + 1], (share, LANES))
                picked = jnp.take_along_axis(
                    window, jnp.maximum(code, 0), axis=1, mode="promise_in_bounds")
                total = total + jnp.where(code >= 0, picked, 0.0)
            out_ref[:, pl.ds(pl.multiple_of(index * LANES, LANES), LANES)] = total.astype(
                out_ref.dtype)


def gather_updates(cols, leaves, starts, codes, values):
    nodes, share, panel = values[0].shape
    width = codes.shape[0] * LANES // leaves
    out = [jax.ShapeDtypeStruct((share, width), jnp.bfloat16 if step else jnp.float32)
           for step in range(leaves)]
    return pl.pallas_call(
        functools.partial(gather_kernel, cols, leaves),
        in_specs=[pl.BlockSpec(memory_space=SMEM)] + whole_vmem(1 + cols),
        out_specs=whole_vmem(leaves),
        out_shape=out,
        scratch_shapes=[VMEM((nodes, share, cols * panel + 2 * LANES), jnp.float32)],
        name="gather_updates",
    )(starts, codes, *values)


def reduce_kernel(cols, leaves, rhs_ref, own_ref, *refs):
    got_refs, rhs_refs, out_ref = refs[:-cols], refs[-cols:-1], refs[-1]
    share, width = own_ref.shape
    block = rhs_ref.shape[1]
    col = lax.axis_index("col")
    leaf = lax.axis_index("leaf")
    total = own_ref[...]
    for ref in got_refs:
        total = total + ref[...].astype(jnp.float32)
    mine = pl.ds(pl.multiple_of(col * share, share), share)
    count = max(1, width // block)
    span = min(width, block)
    for index in range(count):
        if width >= block:
            source, start = leaf * count + index, 0
        else:
            ratio = block // width
            source = leaf // ratio
            start = pl.multiple_of(lax.rem(leaf, ratio) * width, width)
        away = lax.rem(col + cols - source, cols)
        right = jnp.where(away == 0, rhs_ref[mine, pl.ds(start, span)].astype(jnp.float32), 0.0)
        for step, ref in enumerate(rhs_refs, 1):
            right = jnp.where(away == step, ref[:, pl.ds(start, span)].astype(jnp.float32), right)
        at = slice(index * span, (index + 1) * span)
        out_ref[:, at] = (right - total[:, at]).astype(out_ref.dtype)


def reduce_root(cols, leaves, rhs_root, own, got, rhs_got):
    return pl.pallas_call(
        functools.partial(reduce_kernel, cols, leaves),
        in_specs=whole_vmem(2 + len(got) + len(rhs_got)),
        out_specs=pl.BlockSpec(memory_space=VMEM),
        out_shape=jax.ShapeDtypeStruct(own.shape, jnp.bfloat16),
        name="reduce_root",
    )(rhs_root, own, *got, *rhs_got)


def sum_kernel(own_ref, *refs):
    *got_refs, out_ref, sent_ref = refs
    total = own_ref[...]
    for ref in got_refs:
        total = total + ref[...].astype(jnp.float32)
    out_ref[...] = total
    sent_ref[...] = total.astype(sent_ref.dtype)


def sum_leaves(own, got):
    return pl.pallas_call(
        sum_kernel,
        in_specs=whole_vmem(1 + len(got)),
        out_specs=whole_vmem(2),
        out_shape=[own, jax.ShapeDtypeStruct(own.shape, jnp.bfloat16)],
        name="sum_leaves",
    )(own, *got)


def send_rhs(cols, leaves, rhs_root):
    share = rhs_root.shape[0] // cols
    col = lax.axis_index("col")
    got = []
    for step in range(1, cols):
        start = lax.rem(col + step, cols) * share
        piece = lax.dynamic_slice_in_dim(rhs_root, start, share, 0)
        pairs = []
        for leaf in range(leaves):
            for source in range(leaf * cols // leaves, max(leaf * cols // leaves + 1, (leaf + 1) * cols // leaves)):
                pairs.append((leaf * cols + source, leaf * cols + (source + step) % cols))
        got.append(lax.ppermute(piece, ("leaf", "col"), pairs))
    return got


def index_tables(row_index, width):
    tiles = width // LANES
    rows = row_index.shape[1]
    high, low = row_index // LANES, row_index % LANES
    in_tile = high[:, None, :] == lax.iota(jnp.int32, tiles)[None, :, None]
    number = (lax.iota(jnp.int32, rows) % LANES).astype(jnp.bfloat16)
    is_lane = (low[:, :, None] == lax.iota(jnp.int32, LANES)).astype(jnp.bfloat16)
    left = jnp.stack([jnp.where(in_tile, number, 0), in_tile.astype(jnp.bfloat16)], 1)
    both = jnp.einsum("kntp,kpl->ntkl", left, is_lane, preferred_element_type=jnp.float32)
    codes = jnp.where(both[1] > 0.5, both[0], -1.0).astype(jnp.int32)
    before = high[:, None, :] < lax.iota(jnp.int32, tiles)[None, :, None]
    starts = jnp.sum(before.astype(jnp.int32), axis=2)
    return starts, codes


def local(rhs_leaf, dinv_leaf, panel_leaf, counts, row_index, rhs_root, dinv_root):
    cols, rows, leaves = (lax.axis_size(name) for name in ("col", "row", "leaf"))
    width = rhs_root.shape[1] * cols
    leaf = lax.axis_index("leaf")

    rhs_got = send_rhs(cols, leaves, rhs_root)
    partials = leaf_partials(cols, counts, rhs_leaf[0], dinv_leaf[0])
    got = [shift(partials[step], "col", step) for step in range(1, cols)]
    starts, codes = index_tables(row_index[0], width)
    solved = solve_rows(counts, partials[0], got)
    pieces = [solved] + [shift(solved, "col", step) for step in range(1, cols)]
    updates = []
    for step, piece in enumerate(pieces):
        update = jnp.einsum("kbi,kri->kbr", piece, panel_leaf[0], preferred_element_type=jnp.float32)
        if step:
            update = shift(update.astype(jnp.bfloat16), "col", cols - step)
        updates.append(update)
    y_leaf = join_columns(pieces)

    sums = gather_updates(cols, leaves, starts, codes, updates)
    sums_got = [shift(sums[step], "leaf", step) for step in range(1, leaves)]
    own, sent = sum_leaves(sums[0], sums_got)
    got = [shift(sent, "row", step) for step in range(1, rows)]
    reduced = reduce_root(cols, leaves, rhs_root, own, got, rhs_got)
    part = width // leaves
    total = 0.0
    for step in range(leaves):
        piece = shift(reduced, "leaf", step) if step else reduced
        block = lax.rem(leaf + leaves - step, leaves)
        inverse = lax.dynamic_slice_in_dim(dinv_root, block * part, part, 1)
        total = total + lax.dot_general(piece, inverse, NT, preferred_element_type=jnp.float32)
    mine = total.astype(jnp.bfloat16)
    y_root = join_columns([mine] + [shift(mine, "col", step) for step in range(1, cols)])
    return y_leaf[None], y_root


def solution(mesh):
    in_specs = (
        P("leaf", None, None, "col"),
        P("leaf", None, "row", "col"),
        P("leaf", None, "col", "row"),
        P("leaf", None),
        P("leaf", None, None),
        P(None, "col"),
        P(("leaf", "row"), None),
    )
    out_specs = (P("leaf", None, None, "row"), P(None, ("leaf", "row")))
    return jax.shard_map(local, mesh=mesh, in_specs=in_specs, out_specs=out_specs, check_vma=False)
```

time: 219 us -> 91.5 us (0.42)
  waiting for transfers between devices: 153 us -> 17.8 us
  starting transfers between devices: 0.12 us -> 35.2 us
  blocking collectives: 22.4 us -> 0 us
  Pallas kernels: 0 us -> 21.3 us
  other arithmetic: 16.2 us -> 1.76 us
  between operations: 13.8 us -> 0.9 us
    psum x2 -> x0, waiting for transfers between devices: 110 us -> none  [the longest x1 56.2 us: local(): share = lax.psum(piece, ('leaf', 'row'))]
    reduce_scatter x1 -> x0, waiting for transfers between devices: 42.8 us -> none  [local(): piece = lax.psum_scatter(accum, 'col', scatter_dimension=1, tiled=True)]
    ppermute x0 -> x20, starting transfers between devices: none -> 35.2 us  [the longest x17 28 us: shift(): return lax.ppermute(value, axis, pairs)]
    all_gather x1 -> x0, blocking collectives: 22.4 us -> none  [local(): whole_reduced = lax.all_gather(reduced, 'col', axis=1, tiled=True)]
    pallas_call x0 -> x7, Pallas kernels: none -> 21.3 us  [the longest x1 6.98 us: leaf_partials(): pl.pallas_call(functools.partial(leaf_kernel, cols), grid=(nodes,), in_sp...]
    ppermute x0 -> x20, waiting for transfers between devices: none -> 17.8 us  [the longest x17 16.3 us: shift(): return lax.ppermute(value, axis, pairs)]
    scatter-add x1 -> x0, other arithmetic: 13.3 us -> none  [local(): jnp.zeros((columns, sep_width), jnp.float32).at[:, targets.reshape(-1)]]
    unnamed x9 -> x50, local copies, waits for them, and re-layouts: 0.9 us -> 3.35 us
  transfers between devices with their start and end apart: 3 -> 20, of which waited for: 3 -> 9; matrix products, arithmetic and copies ran while one was open for 1% -> 9% of each run, Pallas kernels for 0% -> 4%
where the time goes in v1:
time: 91.5 us; the launch traced here: 91 us
  starting transfers between devices  35.2 us (38%)
  Pallas kernels  21.3 us (23%)
  waiting for transfers between devices  17.8 us (19%)
  matrix products  10.5 us (11%)
  local copies, waits for them, and re-layouts  3.53 us (4%)
  other arithmetic  1.76 us (2%)
    ppermute x17, starting transfers between devices, shift(): return lax.ppermute(value, axis, pairs)  28 us
    ppermute x17, waiting for transfers between devices, shift(): return lax.ppermute(value, axis, pairs)  16.3 us
    ppermute x3, starting transfers between devices, send_rhs(): got.append(lax.ppermute(piece, ('leaf', 'col'), pairs))  7.12 us
    pallas_call x1, Pallas kernels, leaf_partials(): pl.pallas_call(functools.partial(leaf_kernel, cols), grid=(nodes,), in_sp...  6.98 us
    pallas_call x1, Pallas kernels, gather_updates(): pl.pallas_call(functools.partial(gather_kernel, cols, leaves), in_specs=[...  5.79 us
    dot_general x2, matrix products, local(): lax.dot_general(piece, inverse, NT, preferred_element_type=jnp.float32)  4.48 us
    unnamed x50, local copies, waits for them, and re-layouts  3.35 us
    pallas_call x2, Pallas kernels, join_columns(): pl.pallas_call(functools.partial(join_kernel, 0), in_specs=whole_vmem(len...  3.34 us
  transfers between devices with their start and end apart: 20, of which 9 were waited for; matrix products, arithmetic and copies ran while one was open for 9% of the time, Pallas kernels for 4%

profile of v1, /device:TPU:0, one launch (start us, length us, event | category | flops | bytes accessed | tf_op | source)
XLA Modules:
  0.0 91.0 jit_solution(14140182381872762204)
XLA Ops:
  0.7 7.0 %leaf_partials.1 = (f32[8,16,512]{2,1,0:T(8,128)}, bf16[8,16,512]{2,1,0:T(8,128)(2,1)}, bf16[8,16,512]{2,1,0:T(8,128)(2,1)}, bf16[8,16,512]{2,1,0:T(8,128)(2,1)}) custom-call(s32[1,8]{1,0:T(1,128)} %counts_ref.3, bf16[8,64,512]{2,1,0:T(8,128)(2,1)} %bitcast.62, bf16[8,512,512]{2,1,0:T(8,128)(2,1)} %bitcast.60), custom_call_target="tpu_custom_call" | custom-call | flops 268435456 | bytes 4194304 | tf_op jit(solution)/shard_map/leaf_partials/pallas_call | solution.py:46
  7.6 3.1 %collective-permute-start = (bf16[8,16,512]{2,1,0:T(8,128)(2,1)}, bf16[8,16,512]{2,1,0:T(8,128)(2,1)S(1)}, u32[]{:S(2)}, u32[]{:S(2)}) collective-permute-start(bf16[8,16,512]{2,1,0:T(8,128)(2,1)} %get-tuple-element.11), channel_id=1, source_target_pairs={{0,1},{1,2},{2,3},{3,0},{4,5},{5,6},{6,7},{7,4},{8,9},{9,10},{10,1... | collective-permute-start | bytes 393224 | tf_op jit(solution)/shard_map/ppermute | solution.py:19
  10.7 2.6 %collective-permute-start.1 = (bf16[8,16,512]{2,1,0:T(8,128)(2,1)}, bf16[8,16,512]{2,1,0:T(8,128)(2,1)S(1)}, u32[]{:S(2)}, u32[]{:S(2)}) collective-permute-start(bf16[8,16,512]{2,1,0:T(8,128)(2,1)} %get-tuple-element.12), channel_id=1, source_target_pairs={{0,2},{1,3},{2,0},{3,1},{4,6},{5,7},{6,4},{7,5},{8,10},{9,11},{10,... | collective-permute-start | bytes 393224 | tf_op jit(solution)/shard_map/ppermute | solution.py:19
  15.0 2.8 %fusion.1 = f32[8,128,2,32]{1,3,2,0:T(8,128)S(1)} fusion(s32[8,1024]{1,0:T(8,128)S(1)} %get-tuple-element.21, bf16[8,1,32,1024]{3,2,1,0:T(8,128)(2,1)S(1)} %fusion.34, bf16[8,1,32,1024]{3,2,1,0:T(8,128)(2,1)S(1)} %fusion.35), kind=kOutput, calls=%fused_computation.2 | convolution fusion | flops 137363456 | bytes 1343488 | tf_op jit(solution)/shard_map/kntp,kpl->ntkl/dot_general | solution.py:242
  18.0 4.2 %collective-permute-done.1.refs_1_ = bf16[8,16,512]{2,1,0:T(8,128)(2,1)S(1)} collective-permute-done((bf16[8,16,512]{2,1,0:T(8,128)(2,1)}, bf16[8,16,512]{2,1,0:T(8,128)(2,1)S(1)}, u32[]{:S(2)}, u32[]{:S(2)}) %collective-permute-start.1) | collective-permute-done | bytes 131104 | tf_op jit(solution)/shard_map/ppermute | solution.py:19
  22.9 1.8 %solve_rows.1.refs_0_ = bf16[8,16,512]{2,1,0:T(8,128)(2,1)} custom-call(s32[1,8]{1,0:T(1,128)} %counts_ref.3, f32[8,16,512]{2,1,0:T(8,128)} %get-tuple-element.10.own_ref, bf16[8,16,512]{2,1,0:T(8,128)(2,1)} %copy-done.7, bf16[8,16,512]{2,1,0:T(8,128)(2,1)} %copy-done.8, bf16[8,16,512]{2,1,0:T(8,128)(2,1)} %copy-done.9), custom_call_target="tpu_custom_call" | custom-call | tf_op jit(solution)/shard_map/solve_rows/pallas_call | solution.py:81
  24.7 4.3 %collective-permute-start.5 = (bf16[8,16,512]{2,1,0:T(8,128)(2,1)}, bf16[8,16,512]{2,1,0:T(8,128)(2,1)S(1)}, u32[]{:S(2)}, u32[]{:S(2)}) collective-permute-start(bf16[8,16,512]{2,1,0:T(8,128)(2,1)} %solve_rows.1.refs_0_), channel_id=1, source_target_pairs={{0,3},{1,0},{2,1},{3,2},{4,7},{5,4},{6,5},{7,6},{8,11},{9,8},{10,9... | collective-permute-start | bytes 393224 | tf_op jit(solution)/shard_map/ppermute | solution.py:19
  31.2 1.6 %collective-permute-done.5.refs_3_ = bf16[8,16,512]{2,1,0:T(8,128)(2,1)S(1)} collective-permute-done((bf16[8,16,512]{2,1,0:T(8,128)(2,1)}, bf16[8,16,512]{2,1,0:T(8,128)(2,1)S(1)}, u32[]{:S(2)}, u32[]{:S(2)}) %collective-permute-start.5) | collective-permute-done | bytes 131104 | tf_op jit(solution)/shard_map/ppermute | solution.py:19
  33.4 8.2 %collective-permute-start.8 = (bf16[8,16,256]{2,1,0:T(8,128)(2,1)S(1)}, bf16[8,16,256]{2,1,0:T(8,128)(2,1)S(1)}, u32[]{:S(2)}, u32[]{:S(2)}) collective-permute-start(bf16[8,16,256]{2,1,0:T(8,128)(2,1)S(1)} %fusion.22), channel_id=1, source_target_pairs={{0,1},{1,2},{2,3},{3,0},{4,5},{5,6},{6,7},{7,4},{8,9},{9,10},{10,1... | collective-permute-start | bytes 196616 | tf_op jit(solution)/shard_map/ppermute | solution.py:19
  41.6 2.0 %collective-permute-done.4.refs_2_ = bf16[8,16,512]{2,1,0:T(8,128)(2,1)S(1)} collective-permute-done((bf16[8,16,512]{2,1,0:T(8,128)(2,1)}, bf16[8,16,512]{2,1,0:T(8,128)(2,1)S(1)}, u32[]{:S(2)}, u32[]{:S(2)}) %collective-permute-start.4) | collective-permute-done | bytes 131104 | tf_op jit(solution)/shard_map/ppermute | solution.py:19
  46.7 3.0 %collective-permute-done.7.refs_2_ = bf16[8,16,256]{2,1,0:T(8,128)(2,1)S(1)} collective-permute-done((bf16[8,16,256]{2,1,0:T(8,128)(2,1)S(1)}, bf16[8,16,256]{2,1,0:T(8,128)(2,1)S(1)}, u32[]{:S(2)}, u32[]{:S(2)}) %collective-permute-start.7) | collective-permute-done | bytes 65568 | tf_op jit(solution)/shard_map/ppermute | solution.py:19
  50.9 5.8 %gather_updates.1 = (f32[16,2048]{1,0:T(8,128)}, bf16[16,2048]{1,0:T(8,128)(2,1)}) custom-call(s32[8,32]{1,0:T(8,128)} %convert_reduce_fusion.starts_ref, s32[32,8,128]{2,1,0:T(8,128)} %fusion.37.code_ref, f32[8,16,256]{2,1,0:T(8,128)} %fusion.9.refs_0_, bf16[8,16,256]{2,1,0:T(8,128)(2,1)} %copy-done.16, bf16[8,16,256]{2,1,0:T(8,128)(2,1)} %copy-done.15, ...), custom_call_target="tpu_custom_call" | custom-call | tf_op jit(solution)/shard_map/gather_updates/pallas_call | solution.py:153
  56.7 3.2 %collective-permute-start.15 = (bf16[16,1024]{1,0:T(8,128)(2,1)S(1)}, bf16[16,1024]{1,0:T(8,128)(2,1)S(1)}, u32[]{:S(2)}, u32[]{:S(2)}) collective-permute-start(bf16[16,1024]{1,0:T(8,128)(2,1)S(1)} %get-tuple-element.18), channel_id=1, source_target_pairs={{0,3},{1,0},{18,17},{19,18},{4,7},{5,4},{22,21},{23,22},{8,11},{9,... | collective-permute-start | bytes 98312 | tf_op jit(solution)/shard_map/ppermute | solution.py:230
  60.6 1.6 %sum_leaves.1 = (f32[16,2048]{1,0:T(8,128)}, bf16[16,2048]{1,0:T(8,128)(2,1)}) custom-call(f32[16,2048]{1,0:T(8,128)} %get-tuple-element.14.own_ref, bf16[16,2048]{1,0:T(8,128)(2,1)} %copy-done.17), custom_call_target="tpu_custom_call" | custom-call | tf_op jit(solution)/shard_map/sum_leaves/pallas_call | solution.py:210
  62.2 2.4 %collective-permute-start.12 = (bf16[16,2048]{1,0:T(8,128)(2,1)}, bf16[16,2048]{1,0:T(8,128)(2,1)S(1)}, u32[]{:S(2)}, u32[]{:S(2)}) collective-permute-start(bf16[16,2048]{1,0:T(8,128)(2,1)} %get-tuple-element.17), channel_id=1, source_target_pairs={{0,12},{4,0},{8,4},{12,8},{1,13},{5,1},{9,5},{13,9},{2,14},{6,2},{... | collective-permute-start | bytes 196616 | tf_op jit(solution)/shard_map/ppermute | solution.py:19
  65.7 2.0 %collective-permute-start.14 = (bf16[16,1024]{1,0:T(8,128)(2,1)S(1)}, bf16[16,1024]{1,0:T(8,128)(2,1)S(1)}, u32[]{:S(2)}, u32[]{:S(2)}) collective-permute-start(bf16[16,1024]{1,0:T(8,128)(2,1)S(1)} %get-tuple-element.19), channel_id=1, source_target_pairs={{0,2},{1,3},{18,16},{19,17},{4,6},{5,7},{22,20},{23,21},{8,10},{9,... | collective-permute-start | bytes 98312 | tf_op jit(solution)/shard_map/ppermute | solution.py:230
  67.7 2.0 %collective-permute-start.13 = (bf16[16,1024]{1,0:T(8,128)(2,1)S(1)}, bf16[16,1024]{1,0:T(8,128)(2,1)S(1)}, u32[]{:S(2)}, u32[]{:S(2)}) collective-permute-start(bf16[16,1024]{1,0:T(8,128)(2,1)S(1)} %get-tuple-element.20), channel_id=1, source_target_pairs={{0,1},{1,2},{18,19},{19,16},{4,5},{5,6},{22,23},{23,20},{8,9},{9,1... | collective-permute-start | bytes 98312 | tf_op jit(solution)/shard_map/ppermute | solution.py:230
  69.7 1.6 %collective-permute-done.13.refs_3_ = bf16[16,1024]{1,0:T(8,128)(2,1)S(1)} collective-permute-done((bf16[16,1024]{1,0:T(8,128)(2,1)S(1)}, bf16[16,1024]{1,0:T(8,128)(2,1)S(1)}, u32[]{:S(2)}, u32[]{:S(2)}) %collective-permute-start.13) | collective-permute-done | bytes 32800 | tf_op jit(solution)/shard_map/ppermute | solution.py:230
  71.9 1.7 %reduce_root.1 = bf16[16,2048]{1,0:T(8,128)(2,1)} custom-call(bf16[64,1024]{1,0:T(8,128)(2,1)} %rhs_ref.1, f32[16,2048]{1,0:T(8,128)} %get-tuple-element.16.own_ref, bf16[16,2048]{1,0:T(8,128)(2,1)} %copy-done.13, bf16[16,2048]{1,0:T(8,128)(2,1)} %copy-done.12, bf16[16,2048]{1,0:T(8,128)(2,1)} %copy-done.11, bf16[16,1024]{1,0:T(8,128)(2,1)} %copy-done.21, ...), custom_call_target="tpu_custom_call" | custom-call | tf_op jit(solution)/shard_map/reduce_root/pallas_call | solution.py:191
  75.1 2.2 %fusion.11 = f32[16,512]{1,0:T(8,128)S(1)} fusion(bf16[16,2048]{1,0:T(8,128)(2,1)S(1)} %collective-permute-done.16, bf16[512,4096]{1,0:T(8,128)(2,1)} %param.13, s32[]{:T(128)S(6)} %select_n.66), kind=kOutput, calls=%fused_computation.11 | convolution fusion | flops 33554432 | bytes 2195460 | tf_op jit(solution)/shard_map/dot_general | solution.py:279
  77.4 2.3 %fusion.28.refs_0_ = bf16[16,512]{1,0:T(8,128)(2,1)S(1)} fusion(f32[16,512]{1,0:T(8,128)S(1)} %fusion.11, bf16[16,2048]{1,0:T(8,128)(2,1)S(1)} %copy-done.6, bf16[512,4096]{1,0:T(8,128)(2,1)} %param.13, s32[]{:T(128)S(6)} %select_n.65), kind=kOutput, calls=%fused_computation.20 | convolution fusion | flops 33570816 | bytes 2211844 | tf_op jit(solution)/shard_map/dot_general | solution.py:279
  81.1 2.3 %collective-permute-start.18 = (bf16[16,512]{1,0:T(8,128)(2,1)S(1)}, bf16[16,512]{1,0:T(8,128)(2,1)S(1)}, u32[]{:S(2)}, u32[]{:S(2)}) collective-permute-start(bf16[16,512]{1,0:T(8,128)(2,1)S(1)} %fusion.28.refs_0_), channel_id=1, source_target_pairs={{0,2},{1,3},{2,0},{3,1},{4,6},{5,7},{6,4},{7,5},{8,10},{9,11},{10,... | collective-permute-start | bytes 49160 | tf_op jit(solution)/shard_map/ppermute | solution.py:19
  83.4 1.9 %join_columns.2 = bf16[8,64,512]{2,1,0:T(8,128)(2,1)} custom-call(bf16[8,16,512]{2,1,0:T(8,128)(2,1)} %solve_rows.1.refs_0_, bf16[8,16,512]{2,1,0:T(8,128)(2,1)} %copy-done.4, bf16[8,16,512]{2,1,0:T(8,128)(2,1)} %copy-done.3, bf16[8,16,512]{2,1,0:T(8,128)(2,1)} %copy-done.2), custom_call_target="tpu_custom_call" | custom-call | tf_op jit(solution)/shard_map/join_columns/pallas_call | solution.py:106
  85.8 3.2 %collective-permute-done.17.refs_1_ = bf16[16,512]{1,0:T(8,128)(2,1)S(1)} collective-permute-done((bf16[16,512]{1,0:T(8,128)(2,1)S(1)}, bf16[16,512]{1,0:T(8,128)(2,1)S(1)}, u32[]{:S(2)}, u32[]{:S(2)}) %collective-permute-start.17) | collective-permute-done | bytes 16416 | tf_op jit(solution)/shard_map/ppermute | solution.py:19
  (88 shorter events, 17.3 us)
Async XLA Ops:
  0.6 32.1 %copy-start = (bf16[1,8,256,512]{3,2,1,0:T(8,128)(2,1)S(1)}, bf16[1,8,256,512]{3,2,1,0:T(8,128)(2,1)}, u32[]{:S(2)}) copy-start(bf16[1,8,256,512]{3,2,1,0:T(8,128)(2,1)} %param.9) | copy-start | bytes 6291460
  0.6 14.0 %copy-start.18 = (s32[1,8,1024]{2,1,0:T(8,128)S(1)}, s32[1,8,1024]{2,1,0:T(8,128)}, u32[]{:S(2)}) copy-start(s32[1,8,1024]{2,1,0:T(8,128)} %param.11) | copy-start | bytes 98308
  7.6 10.3 %collective-permute-start = (bf16[8,16,512]{2,1,0:T(8,128)(2,1)}, bf16[8,16,512]{2,1,0:T(8,128)(2,1)S(1)}, u32[]{:S(2)}, u32[]{:S(2)}) collective-permute-start(bf16[8,16,512]{2,1,0:T(8,128)(2,1)} %get-tuple-element.11), channel_id=1, source_target_pairs={{0,1},{1,2},{2,3},{3,0},{4,5},{5,6},{6,7},{7,4},{8,9},{9,10},{10,1... | collective-permute-start | bytes 393224 | tf_op jit(solution)/shard_map/ppermute | solution.py:19
  10.7 11.4 %collective-permute-start.1 = (bf16[8,16,512]{2,1,0:T(8,128)(2,1)}, bf16[8,16,512]{2,1,0:T(8,128)(2,1)S(1)}, u32[]{:S(2)}, u32[]{:S(2)}) collective-permute-start(bf16[8,16,512]{2,1,0:T(8,128)(2,1)} %get-tuple-element.12), channel_id=1, source_target_pairs={{0,2},{1,3},{2,0},{3,1},{4,6},{5,7},{6,4},{7,5},{8,10},{9,11},{10,... | collective-permute-start | bytes 393224 | tf_op jit(solution)/shard_map/ppermute | solution.py:19
  13.3 8.9 %collective-permute-start.2 = (bf16[8,16,512]{2,1,0:T(8,128)(2,1)}, bf16[8,16,512]{2,1,0:T(8,128)(2,1)S(1)}, u32[]{:S(2)}, u32[]{:S(2)}) collective-permute-start(bf16[8,16,512]{2,1,0:T(8,128)(2,1)} %get-tuple-element.13), channel_id=1, source_target_pairs={{0,3},{1,0},{2,1},{3,2},{4,7},{5,4},{6,5},{7,6},{8,11},{9,8},{10,9... | collective-permute-start | bytes 393224 | tf_op jit(solution)/shard_map/ppermute | solution.py:19
  24.7 8.0 %collective-permute-start.5 = (bf16[8,16,512]{2,1,0:T(8,128)(2,1)}, bf16[8,16,512]{2,1,0:T(8,128)(2,1)S(1)}, u32[]{:S(2)}, u32[]{:S(2)}) collective-permute-start(bf16[8,16,512]{2,1,0:T(8,128)(2,1)} %solve_rows.1.refs_0_), channel_id=1, source_target_pairs={{0,3},{1,0},{2,1},{3,2},{4,7},{5,4},{6,5},{7,6},{8,11},{9,8},{10,9... | collective-permute-start | bytes 393224 | tf_op jit(solution)/shard_map/ppermute | solution.py:19
  30.6 13.0 %collective-permute-start.4 = (bf16[8,16,512]{2,1,0:T(8,128)(2,1)}, bf16[8,16,512]{2,1,0:T(8,128)(2,1)S(1)}, u32[]{:S(2)}, u32[]{:S(2)}) collective-permute-start(bf16[8,16,512]{2,1,0:T(8,128)(2,1)} %solve_rows.1.refs_0_), channel_id=1, source_target_pairs={{0,2},{1,3},{2,0},{3,1},{4,6},{5,7},{6,4},{7,5},{8,10},{9,11},{10,... | collective-permute-start | bytes 393224 | tf_op jit(solution)/shard_map/ppermute | solution.py:19
  30.9 13.4 %collective-permute-start.3 = (bf16[8,16,512]{2,1,0:T(8,128)(2,1)}, bf16[8,16,512]{2,1,0:T(8,128)(2,1)S(1)}, u32[]{:S(2)}, u32[]{:S(2)}) collective-permute-start(bf16[8,16,512]{2,1,0:T(8,128)(2,1)} %solve_rows.1.refs_0_), channel_id=1, source_target_pairs={{0,1},{1,2},{2,3},{3,0},{4,5},{5,6},{6,7},{7,4},{8,9},{9,10},{10,1... | collective-permute-start | bytes 393224 | tf_op jit(solution)/shard_map/ppermute | solution.py:19
  33.4 12.0 %copy-start.1 = (bf16[8,16,512]{2,1,0:T(8,128)(2,1)S(1)}, bf16[8,16,512]{2,1,0:T(8,128)(2,1)}, u32[]{:S(2)}) copy-start(bf16[8,16,512]{2,1,0:T(8,128)(2,1)} %solve_rows.1.refs_0_) | copy-start | bytes 393220
  33.4 13.3 %collective-permute-start.8 = (bf16[8,16,256]{2,1,0:T(8,128)(2,1)S(1)}, bf16[8,16,256]{2,1,0:T(8,128)(2,1)S(1)}, u32[]{:S(2)}, u32[]{:S(2)}) collective-permute-start(bf16[8,16,256]{2,1,0:T(8,128)(2,1)S(1)} %fusion.22), channel_id=1, source_target_pairs={{0,1},{1,2},{2,3},{3,0},{4,5},{5,6},{6,7},{7,4},{8,9},{9,10},{10,1... | collective-permute-start | bytes 196616 | tf_op jit(solution)/shard_map/ppermute | solution.py:19
  44.2 12.5 %copy-start.5 = (bf16[64,1024]{1,0:T(8,128)(2,1)S(1)}, bf16[64,1024]{1,0:T(8,128)(2,1)}, u32[]{:S(2)}) copy-start(bf16[64,1024]{1,0:T(8,128)(2,1)} %rhs_ref.1) | copy-start | bytes 393220
  44.2 5.5 %collective-permute-start.7 = (bf16[8,16,256]{2,1,0:T(8,128)(2,1)S(1)}, bf16[8,16,256]{2,1,0:T(8,128)(2,1)S(1)}, u32[]{:S(2)}, u32[]{:S(2)}) collective-permute-start(bf16[8,16,256]{2,1,0:T(8,128)(2,1)S(1)} %fusion.19), channel_id=1, source_target_pairs={{0,2},{1,3},{2,0},{3,1},{4,6},{5,7},{6,4},{7,5},{8,10},{9,11},{10,... | collective-permute-start | bytes 196616 | tf_op jit(solution)/shard_map/ppermute | solution.py:19
  44.9 5.2 %collective-permute-start.6 = (bf16[8,16,256]{2,1,0:T(8,128)(2,1)S(1)}, bf16[8,16,256]{2,1,0:T(8,128)(2,1)S(1)}, u32[]{:S(2)}, u32[]{:S(2)}) collective-permute-start(bf16[8,16,256]{2,1,0:T(8,128)(2,1)S(1)} %fusion.16), channel_id=1, source_target_pairs={{0,3},{1,0},{2,1},{3,2},{4,7},{5,4},{6,5},{7,6},{8,11},{9,8},{10,9... | collective-permute-start | bytes 196616 | tf_op jit(solution)/shard_map/ppermute | solution.py:19
  56.7 3.2 %collective-permute-start.9 = (bf16[16,2048]{1,0:T(8,128)(2,1)}, bf16[16,2048]{1,0:T(8,128)(2,1)S(1)}, u32[]{:S(2)}, u32[]{:S(2)}) collective-permute-start(bf16[16,2048]{1,0:T(8,128)(2,1)} %get-tuple-element.15), channel_id=1, source_target_pairs={{0,16},{16,0},{1,17},{17,1},{2,18},{18,2},{3,19},{19,3},{4,20},{20... | collective-permute-start | bytes 196616 | tf_op jit(solution)/shard_map/ppermute | solution.py:19
  56.7 10.9 %collective-permute-start.15 = (bf16[16,1024]{1,0:T(8,128)(2,1)S(1)}, bf16[16,1024]{1,0:T(8,128)(2,1)S(1)}, u32[]{:S(2)}, u32[]{:S(2)}) collective-permute-start(bf16[16,1024]{1,0:T(8,128)(2,1)S(1)} %get-tuple-element.18), channel_id=1, source_target_pairs={{0,3},{1,0},{18,17},{19,18},{4,7},{5,4},{22,21},{23,22},{8,11},{9,... | collective-permute-start | bytes 98312 | tf_op jit(solution)/shard_map/ppermute | solution.py:230
  62.2 9.1 %collective-permute-start.12 = (bf16[16,2048]{1,0:T(8,128)(2,1)}, bf16[16,2048]{1,0:T(8,128)(2,1)S(1)}, u32[]{:S(2)}, u32[]{:S(2)}) collective-permute-start(bf16[16,2048]{1,0:T(8,128)(2,1)} %get-tuple-element.17), channel_id=1, source_target_pairs={{0,12},{4,0},{8,4},{12,8},{1,13},{5,1},{9,5},{13,9},{2,14},{6,2},{... | collective-permute-start | bytes 196616 | tf_op jit(solution)/shard_map/ppermute | solution.py:19
  64.6 6.7 %collective-permute-start.11 = (bf16[16,2048]{1,0:T(8,128)(2,1)}, bf16[16,2048]{1,0:T(8,128)(2,1)S(1)}, u32[]{:S(2)}, u32[]{:S(2)}) collective-permute-start(bf16[16,2048]{1,0:T(8,128)(2,1)} %get-tuple-element.17), channel_id=1, source_target_pairs={{0,8},{4,12},{8,0},{12,4},{1,9},{5,13},{9,1},{13,5},{2,10},{6,14},... | collective-permute-start | bytes 196616 | tf_op jit(solution)/shard_map/ppermute | solution.py:19
  65.1 6.2 %collective-permute-start.10 = (bf16[16,2048]{1,0:T(8,128)(2,1)}, bf16[16,2048]{1,0:T(8,128)(2,1)S(1)}, u32[]{:S(2)}, u32[]{:S(2)}) collective-permute-start(bf16[16,2048]{1,0:T(8,128)(2,1)} %get-tuple-element.17), channel_id=1, source_target_pairs={{0,4},{4,8},{8,12},{12,0},{1,5},{5,9},{9,13},{13,1},{2,6},{6,10},{... | collective-permute-start | bytes 196616 | tf_op jit(solution)/shard_map/ppermute | solution.py:19
  65.7 4.0 %collective-permute-start.14 = (bf16[16,1024]{1,0:T(8,128)(2,1)S(1)}, bf16[16,1024]{1,0:T(8,128)(2,1)S(1)}, u32[]{:S(2)}, u32[]{:S(2)}) collective-permute-start(bf16[16,1024]{1,0:T(8,128)(2,1)S(1)} %get-tuple-element.19), channel_id=1, source_target_pairs={{0,2},{1,3},{18,16},{19,17},{4,6},{5,7},{22,20},{23,21},{8,10},{9,... | collective-permute-start | bytes 98312 | tf_op jit(solution)/shard_map/ppermute | solution.py:230
  67.7 3.6 %collective-permute-start.13 = (bf16[16,1024]{1,0:T(8,128)(2,1)S(1)}, bf16[16,1024]{1,0:T(8,128)(2,1)S(1)}, u32[]{:S(2)}, u32[]{:S(2)}) collective-permute-start(bf16[16,1024]{1,0:T(8,128)(2,1)S(1)} %get-tuple-element.20), channel_id=1, source_target_pairs={{0,1},{1,2},{18,19},{19,16},{4,5},{5,6},{22,23},{23,20},{8,9},{9,1... | collective-permute-start | bytes 98312 | tf_op jit(solution)/shard_map/ppermute | solution.py:230
  73.7 1.5 %collective-permute-start.16 = (bf16[16,2048]{1,0:T(8,128)(2,1)}, bf16[16,2048]{1,0:T(8,128)(2,1)S(1)}, u32[]{:S(2)}, u32[]{:S(2)}) collective-permute-start(bf16[16,2048]{1,0:T(8,128)(2,1)} %reduce_root.1), channel_id=1, source_target_pairs={{0,16},{16,0},{1,17},{17,1},{2,18},{18,2},{3,19},{19,3},{4,20},{20... | collective-permute-start | bytes 196616 | tf_op jit(solution)/shard_map/ppermute | solution.py:19
  79.6 5.7 %collective-permute-start.19 = (bf16[16,512]{1,0:T(8,128)(2,1)S(1)}, bf16[16,512]{1,0:T(8,128)(2,1)S(1)}, u32[]{:S(2)}, u32[]{:S(2)}) collective-permute-start(bf16[16,512]{1,0:T(8,128)(2,1)S(1)} %fusion.28.refs_0_), channel_id=1, source_target_pairs={{0,3},{1,0},{2,1},{3,2},{4,7},{5,4},{6,5},{7,6},{8,11},{9,8},{10,9... | collective-permute-start | bytes 49160 | tf_op jit(solution)/shard_map/ppermute | solution.py:19
  81.1 4.6 %collective-permute-start.18 = (bf16[16,512]{1,0:T(8,128)(2,1)S(1)}, bf16[16,512]{1,0:T(8,128)(2,1)S(1)}, u32[]{:S(2)}, u32[]{:S(2)}) collective-permute-start(bf16[16,512]{1,0:T(8,128)(2,1)S(1)} %fusion.28.refs_0_), channel_id=1, source_target_pairs={{0,2},{1,3},{2,0},{3,1},{4,6},{5,7},{6,4},{7,5},{8,10},{9,11},{10,... | collective-permute-start | bytes 49160 | tf_op jit(solution)/shard_map/ppermute | solution.py:19
  83.4 5.5 %collective-permute-start.17 = (bf16[16,512]{1,0:T(8,128)(2,1)S(1)}, bf16[16,512]{1,0:T(8,128)(2,1)S(1)}, u32[]{:S(2)}, u32[]{:S(2)}) collective-permute-start(bf16[16,512]{1,0:T(8,128)(2,1)S(1)} %fusion.28.refs_0_), channel_id=1, source_target_pairs={{0,1},{1,2},{2,3},{3,0},{4,5},{5,6},{6,7},{7,4},{8,9},{9,10},{10,1... | collective-permute-start | bytes 49160 | tf_op jit(solution)/shard_map/ppermute | solution.py:19
  (21 other events, 54.4 us)
